TPU v7x, 128 devices: a whole 4x4x4 slice. The times are simulated.
128 devices in a mesh: row: 8 (over z, core), col: 16 (over y, x).
Axes of the slice: x: 4, y: 4, z: 4, core: 2. Of those that a mesh axis runs over, the one named last changes fastest.
Arguments:
- factor_wide: float32 [2, 8, 1, 16, 512, 512], P(None, 'row', None, 'col'), may hold values from -1 to 2, as said below
- factor_narrow: bfloat16 [2, 8, 1, 16, 512, 512], P(None, 'row', None, 'col'), may hold values from -1 to 2, as said below
- flags: int32 [2, 8, 1, 16], P(None, 'row', None, 'col'), may hold values from 0 to 1
- forward_solution: float32 [1, 16, 512, 128], P(None, 'col'), may hold values from -0.5 to 0.5
- solution_grad: float32 [1, 16, 512, 128], P(None, 'col'), may hold values from -1.8 to 1.8
Outputs:
- rhs_grad: float32 [2, 8, 512, 128], P(None, 'row')
- factor_grad: float32 [2, 8, 1, 16, 512, 512], P(None, 'row', None, 'col')
Inputs may be any that keep to these rules, and one draw needn't show every extreme that they name: `factor_wide`: the diagonal entries of every diagonal tile lie between 1 and 2. `factor_narrow`: the diagonal entries of every diagonal tile lie between 1 and 2.
All inputs are finite; a program needn't handle non-finite values.
Results may differ from a plain program's by a relative error of at most 0.0003.
Values sent between devices are 32-bit elements; how exact they have to be, the bound alone decides.
A program may use at most 64 MiB of HBM per device.

v0:
```python
import jax
import jax.numpy as jnp
from jax import lax
from jax.sharding import PartitionSpec as P

HIGHEST_PRECISION = lax.Precision.HIGHEST


def picked(value, axis, root):
    return lax.dynamic_index_in_dim(lax.all_gather(value, axis), root, 0, keepdims=False)


def from_behind(value, axis, by):
    size = lax.axis_size(axis)
    return lax.ppermute(value, axis, [(i, (i + by) % size) for i in range(size)])


def sent_to_all(value, axis):
    size = lax.axis_size(axis)
    return lax.all_to_all(
        jnp.broadcast_to(value[None], (size, *value.shape)), axis, 0, 0, tiled=True
    )


def taken_together(value, axis):
    return sent_to_all(value, axis).sum(axis=0)


def lower_mask(row_index, col_index, tile_width):
    inner_mask = lax.broadcasted_iota(
        jnp.int32, (tile_width, tile_width), 0
    ) >= lax.broadcasted_iota(jnp.int32, (tile_width, tile_width), 1)
    return (row_index > col_index) | (row_index == col_index) & inner_mask


def body(factor_wide, factor_narrow, flags, forward_solution, solution_grad):
    row_count = lax.axis_size("row")
    col_count = lax.axis_size("col")
    my_row = lax.axis_index("row")
    my_col = lax.axis_index("col")
    local_rows = factor_wide.shape[0]
    local_cols = factor_wide.shape[2]
    tile_width = factor_wide.shape[4]
    rhs_width = forward_solution.shape[3]
    tile_count = local_rows * row_count
    factor_tiles = jnp.where(
        flags[:, 0, :, 0, None, None] == 1,
        factor_narrow[:, 0, :, 0].astype(jnp.float32),
        factor_wide[:, 0, :, 0],
    )
    solution_local = forward_solution[:, 0]
    target_local = solution_grad[:, 0]
    row_index = jnp.arange(local_rows, dtype=jnp.int32) * row_count + my_row
    col_index = jnp.arange(local_cols, dtype=jnp.int32) * col_count + my_col
    empty_block = jnp.zeros((tile_width, rhs_width), jnp.float32)

    def nothing_block():
        return empty_block

    def column_partial(rhs_local, target, lowest):

        def on_owner():
            column = lax.dynamic_index_in_dim(factor_tiles, target // col_count, 1, keepdims=False)
            weight = (row_index >= lowest).astype(jnp.float32)
            masked = rhs_local * weight[:, None, None]
            return jnp.einsum("aki,akr->ir", column, masked, precision=HIGHEST_PRECISION)

        return lax.cond(my_col == target % col_count, on_owner, nothing_block)

    def target_block(target):
        return lax.dynamic_index_in_dim(target_local, target // col_count, 0, keepdims=False)

    def advance(right_side, target, carried):
        rhs_local, factor_grad = carried
        local_slot = target // row_count
        holds_row = my_row == target % row_count
        is_owner = holds_row & (my_col == target % col_count)

        def solve_here():
            tile_row = lax.dynamic_index_in_dim(factor_tiles, local_slot, 0, keepdims=False)
            diagonal = lax.dynamic_index_in_dim(tile_row, target // col_count, 0, keepdims=False)
            return lax.linalg.triangular_solve(
                diagonal, right_side, left_side=True, lower=True, transpose_a=True
            )

        solved = lax.cond(is_owner, solve_here, nothing_block)
        arrived = picked(solved, "col", target % col_count)
        current = lax.dynamic_index_in_dim(rhs_local, local_slot, 0, keepdims=False)
        rhs_local = lax.dynamic_update_index_in_dim(
            rhs_local, jnp.where(holds_row, arrived, current), local_slot, 0
        )
        return (rhs_local, factor_grad)

    final_index = tile_count - 1
    carried = (
        jnp.zeros((local_rows, tile_width, rhs_width), jnp.float32),
        jnp.zeros((local_rows, local_cols, tile_width, tile_width), jnp.float32),
    )
    carried = advance(target_block(jnp.int32(final_index)), jnp.int32(final_index), carried)

    def sweep_step(offset, loop_state):
        carried, early_sum = loop_state
        target = final_index - 1 - offset
        rhs_local = carried[0]
        source = target + 1

        def compute_fresh():
            tile_row = lax.dynamic_index_in_dim(
                factor_tiles, source // row_count, 0, keepdims=False
            )
            tile_now = lax.dynamic_index_in_dim(tile_row, target // col_count, 0, keepdims=False)
            newest = lax.dynamic_index_in_dim(rhs_local, source // row_count, 0, keepdims=False)
            return jnp.dot(
                tile_now.T, newest, precision=HIGHEST_PRECISION, preferred_element_type=jnp.float32
            )

        fresh_owner = (my_row == source % row_count) & (my_col == target % col_count)
        fresh_term = lax.cond(fresh_owner, compute_fresh, nothing_block)
        moved_term = from_behind(fresh_term, "row", -1)
        following = jnp.maximum(target - 1, 0)
        next_partial = column_partial(rhs_local, following, source)
        next_sum = taken_together(next_partial, "row")
        carried = advance(target_block(target) - early_sum - moved_term, target, carried)
        return (carried, next_sum)

    carried, unused_sum = lax.fori_loop(0, final_index, sweep_step, (carried, empty_block))
    rhs_local, factor_grad = carried
    products = -jnp.einsum("akr,blr->abkl", rhs_local, solution_local, precision=HIGHEST_PRECISION)
    masks = lower_mask(row_index[:, None, None, None], col_index[None, :, None, None], tile_width)
    factor_grad = jnp.where(masks, products, jnp.zeros_like(products))
    return (rhs_local[:, None], factor_grad[:, None, :, None])


def solution(mesh):
    placed = (
        P(None, "row", None, "col", None, None),
        P(None, "row", None, "col", None, None),
        P(None, "row", None, "col"),
        P(None, "col", None, None),
        P(None, "col", None, None),
    )
    return jax.shard_map(
        body,
        mesh=mesh,
        in_specs=placed,
        out_specs=(P(None, "row", None, None), P(None, "row", None, "col", None, None)),
        check_vma=False,
    )
```

profile of v0, /device:TPU:10, one launch (start us, length us, event | category | flops | bytes accessed | tf_op | source)
XLA Modules:
  0.0 1883.9 jit_solution(5094315341749670597)
XLA Ops:
  12.0 107.4 %all-gather.9.cloned.1.call-done = f32[8192,128]{1,0:T(8,128)} async-done(((f32[512,128]{1,0:T(8,128)}), f32[8192,128]{1,0:T(8,128)}) %all-gather.9.cloned.1.call-update) | async-done | bytes 4194320 | tf_op jit(solution)/shard_map/all_gather | solution.py:10
  121.2 1751.7 %while.28 = (s32[]{:T(128)}, f32[2,512,128]{2,1,0:T(8,128)S(1)}, f32[512,128]{1,0:T(8,128)}, s32[]{:T(128)}, s32[]{:T(128)}, /*index=5*/f32[2,1,512,512]{3,2,0,1...) while((s32[]{:T(128)}, f32[2,512,128]{2,1,0:T(8,128)S(1)}, ...), condition=%wide.region_10.12_spmd.clone.clone, body=%wide.region_2.11_spmd.clone.clone.sunk | while | flops 1461305472 | bytes 40111664 | solution.py:126
  135.9 27.3 %all-to-all-done = f32[8,512,128]{2,1,0:T(8,128)} async-done(((f32[8,512,128]{2,1,0:T(8,128)}), f32[8,512,128]{2,1,0:T(8,128)}, u32[]{:S(2)}, u32[]{:S(2)}) %all-to-all-start) | async-done | bytes 2097184 | tf_op jit(solution)/shard_map/while/body/eval_jaxpr/all_to_all | solution.py:20
  165.6 71.6 %all-gather.11.cloned.1.call-done = f32[8192,128]{1,0:T(8,128)} async-done(((f32[512,128]{1,0:T(8,128)}), f32[8192,128]{1,0:T(8,128)}) %all-gather.11.cloned.1.call-update) | async-done | bytes 4194320 | tf_op jit(solution)/shard_map/while/body/eval_jaxpr/all_gather | solution.py:10
  253.1 27.3 %all-to-all-done = f32[8,512,128]{2,1,0:T(8,128)} async-done(((f32[8,512,128]{2,1,0:T(8,128)}), f32[8,512,128]{2,1,0:T(8,128)}, u32[]{:S(2)}, u32[]{:S(2)}) %all-to-all-start) | async-done | bytes 2097184 | tf_op jit(solution)/shard_map/while/body/eval_jaxpr/all_to_all | solution.py:20
  282.7 73.7 %all-gather.11.cloned.1.call-done = f32[8192,128]{1,0:T(8,128)} async-done(((f32[512,128]{1,0:T(8,128)}), f32[8192,128]{1,0:T(8,128)}) %all-gather.11.cloned.1.call-update) | async-done | bytes 4194320 | tf_op jit(solution)/shard_map/while/body/eval_jaxpr/all_gather | solution.py:10
  372.2 27.3 %all-to-all-done = f32[8,512,128]{2,1,0:T(8,128)} async-done(((f32[8,512,128]{2,1,0:T(8,128)}), f32[8,512,128]{2,1,0:T(8,128)}, u32[]{:S(2)}, u32[]{:S(2)}) %all-to-all-start) | async-done | bytes 2097184 | tf_op jit(solution)/shard_map/while/body/eval_jaxpr/all_to_all | solution.py:20
  401.9 70.9 %all-gather.11.cloned.1.call-done = f32[8192,128]{1,0:T(8,128)} async-done(((f32[512,128]{1,0:T(8,128)}), f32[8192,128]{1,0:T(8,128)}) %all-gather.11.cloned.1.call-update) | async-done | bytes 4194320 | tf_op jit(solution)/shard_map/while/body/eval_jaxpr/all_gather | solution.py:10
  488.7 27.3 %all-to-all-done = f32[8,512,128]{2,1,0:T(8,128)} async-done(((f32[8,512,128]{2,1,0:T(8,128)}), f32[8,512,128]{2,1,0:T(8,128)}, u32[]{:S(2)}, u32[]{:S(2)}) %all-to-all-start) | async-done | bytes 2097184 | tf_op jit(solution)/shard_map/while/body/eval_jaxpr/all_to_all | solution.py:20
  518.3 73.6 %all-gather.11.cloned.1.call-done = f32[8192,128]{1,0:T(8,128)} async-done(((f32[512,128]{1,0:T(8,128)}), f32[8192,128]{1,0:T(8,128)}) %all-gather.11.cloned.1.call-update) | async-done | bytes 4194320 | tf_op jit(solution)/shard_map/while/body/eval_jaxpr/all_gather | solution.py:10
  607.8 27.3 %all-to-all-done = f32[8,512,128]{2,1,0:T(8,128)} async-done(((f32[8,512,128]{2,1,0:T(8,128)}), f32[8,512,128]{2,1,0:T(8,128)}, u32[]{:S(2)}, u32[]{:S(2)}) %all-to-all-start) | async-done | bytes 2097184 | tf_op jit(solution)/shard_map/while/body/eval_jaxpr/all_to_all | solution.py:20
  637.4 70.5 %all-gather.11.cloned.1.call-done = f32[8192,128]{1,0:T(8,128)} async-done(((f32[512,128]{1,0:T(8,128)}), f32[8192,128]{1,0:T(8,128)}) %all-gather.11.cloned.1.call-update) | async-done | bytes 4194320 | tf_op jit(solution)/shard_map/while/body/eval_jaxpr/all_gather | solution.py:10
  753.5 71.6 %all-gather.11.cloned.1.call-done = f32[8192,128]{1,0:T(8,128)} async-done(((f32[512,128]{1,0:T(8,128)}), f32[8192,128]{1,0:T(8,128)}) %all-gather.11.cloned.1.call-update) | async-done | bytes 4194320 | tf_op jit(solution)/shard_map/while/body/eval_jaxpr/all_gather | solution.py:10
  841.0 27.3 %all-to-all-done = f32[8,512,128]{2,1,0:T(8,128)} async-done(((f32[8,512,128]{2,1,0:T(8,128)}), f32[8,512,128]{2,1,0:T(8,128)}, u32[]{:S(2)}, u32[]{:S(2)}) %all-to-all-start) | async-done | bytes 2097184 | tf_op jit(solution)/shard_map/while/body/eval_jaxpr/all_to_all | solution.py:20
  870.6 70.7 %all-gather.11.cloned.1.call-done = f32[8192,128]{1,0:T(8,128)} async-done(((f32[512,128]{1,0:T(8,128)}), f32[8192,128]{1,0:T(8,128)}) %all-gather.11.cloned.1.call-update) | async-done | bytes 4194320 | tf_op jit(solution)/shard_map/while/body/eval_jaxpr/all_gather | solution.py:10
  957.2 27.3 %all-to-all-done = f32[8,512,128]{2,1,0:T(8,128)} async-done(((f32[8,512,128]{2,1,0:T(8,128)}), f32[8,512,128]{2,1,0:T(8,128)}, u32[]{:S(2)}, u32[]{:S(2)}) %all-to-all-start) | async-done | bytes 2097184 | tf_op jit(solution)/shard_map/while/body/eval_jaxpr/all_to_all | solution.py:20
  986.9 72.9 %all-gather.11.cloned.1.call-done = f32[8192,128]{1,0:T(8,128)} async-done(((f32[512,128]{1,0:T(8,128)}), f32[8192,128]{1,0:T(8,128)}) %all-gather.11.cloned.1.call-update) | async-done | bytes 4194320 | tf_op jit(solution)/shard_map/while/body/eval_jaxpr/all_gather | solution.py:10
  1106.8 69.1 %all-gather.11.cloned.1.call-done = f32[8192,128]{1,0:T(8,128)} async-done(((f32[512,128]{1,0:T(8,128)}), f32[8192,128]{1,0:T(8,128)}) %all-gather.11.cloned.1.call-update) | async-done | bytes 4194320 | tf_op jit(solution)/shard_map/while/body/eval_jaxpr/all_gather | solution.py:10
  1187.3 65.9 %all-to-all-start = ((f32[8,512,128]{2,1,0:T(8,128)}), f32[8,512,128]{2,1,0:T(8,128)}, u32[]{:S(2)}, u32[]{:S(2)}) async-start(f32[8,512,128]{2,1,0:T(8,128)} %broadcast_in_dim.78), calls=%async_computation | async-start | bytes 4194304 | tf_op jit(solution)/shard_map/while/body/eval_jaxpr/all_to_all | solution.py:20
  1339.4 69.6 %all-gather.11.cloned.1.call-done = f32[8192,128]{1,0:T(8,128)} async-done(((f32[512,128]{1,0:T(8,128)}), f32[8192,128]{1,0:T(8,128)}) %all-gather.11.cloned.1.call-update) | async-done | bytes 4194320 | tf_op jit(solution)/shard_map/while/body/eval_jaxpr/all_gather | solution.py:10
  1454.6 72.7 %all-gather.11.cloned.1.call-done = f32[8192,128]{1,0:T(8,128)} async-done(((f32[512,128]{1,0:T(8,128)}), f32[8192,128]{1,0:T(8,128)}) %all-gather.11.cloned.1.call-update) | async-done | bytes 4194320 | tf_op jit(solution)/shard_map/while/body/eval_jaxpr/all_gather | solution.py:10
  1572.8 69.6 %all-gather.11.cloned.1.call-done = f32[8192,128]{1,0:T(8,128)} async-done(((f32[512,128]{1,0:T(8,128)}), f32[8192,128]{1,0:T(8,128)}) %all-gather.11.cloned.1.call-update) | async-done | bytes 4194320 | tf_op jit(solution)/shard_map/while/body/eval_jaxpr/all_gather | solution.py:10
  1687.9 70.5 %all-gather.11.cloned.1.call-done = f32[8192,128]{1,0:T(8,128)} async-done(((f32[512,128]{1,0:T(8,128)}), f32[8192,128]{1,0:T(8,128)}) %all-gather.11.cloned.1.call-update) | async-done | bytes 4194320 | tf_op jit(solution)/shard_map/while/body/eval_jaxpr/all_gather | solution.py:10
  1803.9 67.9 %all-gather.11.cloned.1.call-done = f32[8192,128]{1,0:T(8,128)} async-done(((f32[512,128]{1,0:T(8,128)}), f32[8192,128]{1,0:T(8,128)}) %all-gather.11.cloned.1.call-update) | async-done | bytes 4194320 | tf_op jit(solution)/shard_map/while/body/eval_jaxpr/all_gather | solution.py:10
  (330 shorter events, 522.0 us)
Async XLA Ops:
  7.2 112.3 %all-gather.9.cloned.1.call-start = ((), (), s32[]{:S(2)}) async-start(), calls=%async_computation.1 | async-start | bytes 4456448 | tf_op jit(solution)/shard_map/all_gather | solution.py:10
  121.2 116.0 %all-gather.11.cloned.1.call-start = ((), (), s32[]{:S(2)}) async-start(), calls=%async_computation.2 | async-start | bytes 4456448 | tf_op jit(solution)/shard_map/while/body/eval_jaxpr/all_gather | solution.py:10
  131.4 31.8 %all-to-all-start = ((f32[8,512,128]{2,1,0:T(8,128)}), f32[8,512,128]{2,1,0:T(8,128)}, u32[]{:S(2)}, u32[]{:S(2)}) async-start(f32[8,512,128]{2,1,0:T(8,128)} %broadcast_in_dim.78), calls=%async_computation | async-start | bytes 4194304 | tf_op jit(solution)/shard_map/while/body/eval_jaxpr/all_to_all | solution.py:20
  238.2 118.2 %all-gather.11.cloned.1.call-start = ((), (), s32[]{:S(2)}) async-start(), calls=%async_computation.2 | async-start | bytes 4456448 | tf_op jit(solution)/shard_map/while/body/eval_jaxpr/all_gather | solution.py:10
  248.5 31.8 %all-to-all-start = ((f32[8,512,128]{2,1,0:T(8,128)}), f32[8,512,128]{2,1,0:T(8,128)}, u32[]{:S(2)}, u32[]{:S(2)}) async-start(f32[8,512,128]{2,1,0:T(8,128)} %broadcast_in_dim.78), calls=%async_computation | async-start | bytes 4194304 | tf_op jit(solution)/shard_map/while/body/eval_jaxpr/all_to_all | solution.py:20
  357.4 115.4 %all-gather.11.cloned.1.call-start = ((), (), s32[]{:S(2)}) async-start(), calls=%async_computation.2 | async-start | bytes 4456448 | tf_op jit(solution)/shard_map/while/body/eval_jaxpr/all_gather | solution.py:10
  367.7 31.8 %all-to-all-start = ((f32[8,512,128]{2,1,0:T(8,128)}), f32[8,512,128]{2,1,0:T(8,128)}, u32[]{:S(2)}, u32[]{:S(2)}) async-start(f32[8,512,128]{2,1,0:T(8,128)} %broadcast_in_dim.78), calls=%async_computation | async-start | bytes 4194304 | tf_op jit(solution)/shard_map/while/body/eval_jaxpr/all_to_all | solution.py:20
  473.8 118.1 %all-gather.11.cloned.1.call-start = ((), (), s32[]{:S(2)}) async-start(), calls=%async_computation.2 | async-start | bytes 4456448 | tf_op jit(solution)/shard_map/while/body/eval_jaxpr/all_gather | solution.py:10
  484.1 31.8 %all-to-all-start = ((f32[8,512,128]{2,1,0:T(8,128)}), f32[8,512,128]{2,1,0:T(8,128)}, u32[]{:S(2)}, u32[]{:S(2)}) async-start(f32[8,512,128]{2,1,0:T(8,128)} %broadcast_in_dim.78), calls=%async_computation | async-start | bytes 4194304 | tf_op jit(solution)/shard_map/while/body/eval_jaxpr/all_to_all | solution.py:20
  592.9 115.0 %all-gather.11.cloned.1.call-start = ((), (), s32[]{:S(2)}) async-start(), calls=%async_computation.2 | async-start | bytes 4456448 | tf_op jit(solution)/shard_map/while/body/eval_jaxpr/all_gather | solution.py:10
  603.3 31.8 %all-to-all-start = ((f32[8,512,128]{2,1,0:T(8,128)}), f32[8,512,128]{2,1,0:T(8,128)}, u32[]{:S(2)}, u32[]{:S(2)}) async-start(f32[8,512,128]{2,1,0:T(8,128)} %broadcast_in_dim.78), calls=%async_computation | async-start | bytes 4194304 | tf_op jit(solution)/shard_map/while/body/eval_jaxpr/all_to_all | solution.py:20
  708.9 116.2 %all-gather.11.cloned.1.call-start = ((), (), s32[]{:S(2)}) async-start(), calls=%async_computation.2 | async-start | bytes 4456448 | tf_op jit(solution)/shard_map/while/body/eval_jaxpr/all_gather | solution.py:10
  826.1 115.2 %all-gather.11.cloned.1.call-start = ((), (), s32[]{:S(2)}) async-start(), calls=%async_computation.2 | async-start | bytes 4456448 | tf_op jit(solution)/shard_map/while/body/eval_jaxpr/all_gather | solution.py:10
  836.4 31.8 %all-to-all-start = ((f32[8,512,128]{2,1,0:T(8,128)}), f32[8,512,128]{2,1,0:T(8,128)}, u32[]{:S(2)}, u32[]{:S(2)}) async-start(f32[8,512,128]{2,1,0:T(8,128)} %broadcast_in_dim.78), calls=%async_computation | async-start | bytes 4194304 | tf_op jit(solution)/shard_map/while/body/eval_jaxpr/all_to_all | solution.py:20
  942.3 117.4 %all-gather.11.cloned.1.call-start = ((), (), s32[]{:S(2)}) async-start(), calls=%async_computation.2 | async-start | bytes 4456448 | tf_op jit(solution)/shard_map/while/body/eval_jaxpr/all_gather | solution.py:10
  952.7 31.8 %all-to-all-start = ((f32[8,512,128]{2,1,0:T(8,128)}), f32[8,512,128]{2,1,0:T(8,128)}, u32[]{:S(2)}, u32[]{:S(2)}) async-start(f32[8,512,128]{2,1,0:T(8,128)} %broadcast_in_dim.78), calls=%async_computation | async-start | bytes 4194304 | tf_op jit(solution)/shard_map/while/body/eval_jaxpr/all_to_all | solution.py:20
  1060.7 115.2 %all-gather.11.cloned.1.call-start = ((), (), s32[]{:S(2)}) async-start(), calls=%async_computation.2 | async-start | bytes 4456448 | tf_op jit(solution)/shard_map/while/body/eval_jaxpr/all_gather | solution.py:10
  1176.9 116.9 %all-gather.11.cloned.1.call-start = ((), (), s32[]{:S(2)}) async-start(), calls=%async_computation.2 | async-start | bytes 4456448 | tf_op jit(solution)/shard_map/while/body/eval_jaxpr/all_gather | solution.py:10
  1187.3 93.2 %all-to-all-start = ((f32[8,512,128]{2,1,0:T(8,128)}), f32[8,512,128]{2,1,0:T(8,128)}, u32[]{:S(2)}, u32[]{:S(2)}) async-start(f32[8,512,128]{2,1,0:T(8,128)} %broadcast_in_dim.78), calls=%async_computation | async-start | bytes 4194304 | tf_op jit(solution)/shard_map/while/body/eval_jaxpr/all_to_all | solution.py:20
  1294.9 114.1 %all-gather.11.cloned.1.call-start = ((), (), s32[]{:S(2)}) async-start(), calls=%async_computation.2 | async-start | bytes 4456448 | tf_op jit(solution)/shard_map/while/body/eval_jaxpr/all_gather | solution.py:10
  1410.1 117.2 %all-gather.11.cloned.1.call-start = ((), (), s32[]{:S(2)}) async-start(), calls=%async_computation.2 | async-start | bytes 4456448 | tf_op jit(solution)/shard_map/while/body/eval_jaxpr/all_gather | solution.py:10
  1528.3 114.1 %all-gather.11.cloned.1.call-start = ((), (), s32[]{:S(2)}) async-start(), calls=%async_computation.2 | async-start | bytes 4456448 | tf_op jit(solution)/shard_map/while/body/eval_jaxpr/all_gather | solution.py:10
  1643.4 115.0 %all-gather.11.cloned.1.call-start = ((), (), s32[]{:S(2)}) async-start(), calls=%async_computation.2 | async-start | bytes 4456448 | tf_op jit(solution)/shard_map/while/body/eval_jaxpr/all_gather | solution.py:10
  1759.4 112.4 %all-gather.11.cloned.1.call-start = ((), (), s32[]{:S(2)}) async-start(), calls=%async_computation.2 | async-start | bytes 4456448 | tf_op jit(solution)/shard_map/while/body/eval_jaxpr/all_gather | solution.py:10
  (56 other events, 3664.1 us)
Sparse Core Ops, SparseCore 0:
  11.4 108.0 all-gather.8
  128.2 108.9 all-gather.10
  245.3 110.9 all-gather.10
  364.5 108.2 all-gather.10
  481.0 110.9 all-gather.10
  600.1 107.7 all-gather.10
  716.1 108.9 all-gather.10
  833.2 108.0 all-gather.10
  949.5 110.1 all-gather.10
  1067.9 107.9 all-gather.10
  1184.1 109.7 all-gather.10
  1302.0 106.9 all-gather.10
  1417.2 110.0 all-gather.10
  1535.4 106.8 all-gather.10
  1650.5 107.7 all-gather.10
  1766.5 105.2 all-gather.10
where the time goes:
time: 1890 us; the launch traced here: 1880 us
  waiting for transfers between devices  1580 us (84%)
  starting transfers between devices  163 us (9%)
  local copies, waits for them, and re-layouts  60.9 us (3%)
  other arithmetic  56 us (3%)
    all_gather x16, waiting for transfers between devices, picked(): lax.all_gather(value, axis)  1110 us
    all_to_all x15, waiting for transfers between devices, sent_to_all(): lax.all_to_all(jnp.broadcast_to(value[None], (size, *value.shape)), axis,...  409 us
    all_to_all x15, starting transfers between devices, sent_to_all(): lax.all_to_all(jnp.broadcast_to(value[None], (size, *value.shape)), axis,...  129 us
    ppermute x15, waiting for transfers between devices, from_behind(): lax.ppermute(value, axis, [(i, (i + by) % size) for i in range(size)])  58.4 us
  transfers between devices with their start and end apart: 46, of which 46 were waited for; matrix products, arithmetic and copies ran while one was open for 5% of the time, Pallas kernels for 0%

commit v1 on v0

v1 whole, which is shorter than its diff:
```python
import functools

import jax
import jax.numpy as jnp
from jax import lax
from jax.experimental import pallas as pl
from jax.experimental.pallas import tpu as pltpu
from jax.sharding import PartitionSpec as P

MESH = pl.DeviceIdType.MESH
F32 = jnp.float32
BF16 = jnp.bfloat16
CHUNKS = 8


def halves(value):
    high = value.astype(BF16)
    return high, (value - high.astype(F32)).astype(BF16)


def mul(a, b):
    return jnp.dot(a, b, preferred_element_type=F32)


def dot3(left, high, low):
    left_high, left_low = halves(left)
    rows = left.shape[0]
    both = mul(jnp.concatenate([left_high, left_low], axis=0), high)
    return both[:rows] + both[rows:] + mul(left_high, low)


def dot_full(left, right):
    left_high, left_low = halves(left)
    right_high, right_low = halves(right)
    return mul(left_high, right_high) + (mul(left_low, right_high) + mul(left_high, right_low))


def kernel(
    sizes,
    flags,
    wide_hbm,
    narrow_hbm,
    x_ref,
    g_ref,
    rhs_hbm,
    grad_hbm,
    wide,
    narrow,
    l_high,
    l_low,
    below,
    w_full,
    w_high,
    w_low,
    v_high,
    v_low,
    g_turned,
    x_high,
    x_low,
    y_buf,
    chain,
    part,
    rhs_out,
    grad_out,
    load_sem,
    store_sem,
    below_send,
    below_recv,
    chain_send,
    chain_recv,
    row_recv,
    x_send,
    y_send,
    part_send,
    part_recv,
):
    n_row, n_col, nx, ny, tile, rhs, chunks = sizes
    n_tiles = 2 * n_row
    width = rhs // chunks
    r = lax.axis_index("row")
    c = lax.axis_index("col")
    x = lax.rem(c, nx)
    y = lax.div(c, nx)
    diag_row = lax.rem(c, n_row)
    diag_slot = lax.div(c, n_row)
    is_diag = r == diag_row

    loads = [
        pltpu.make_async_copy(wide_hbm.at[s], wide.at[s], load_sem.at[s]) for s in range(2)
    ] + [
        pltpu.make_async_copy(narrow_hbm.at[s], narrow.at[s], load_sem.at[2 + s]) for s in range(2)
    ]
    for load in loads:
        load.start()

    barrier = pltpu.get_barrier_semaphore()

    def greet(row, col):
        pl.semaphore_signal(barrier, inc=1, device_id=(row, col), device_id_type=MESH)

    for d in range(1, nx):
        greet(r, y * nx + lax.rem(x + d, nx))
    for d in range(1, ny):
        greet(r, lax.rem(y + d, ny) * nx + x)
    for d in range(1, n_row):
        greet(lax.rem(r + d, n_row), c)
    peers = nx + ny + n_row - 3

    @pl.when(is_diag & (c > 0))
    def _():
        greet(lax.rem(c + n_row - 1, n_row), c - 1)

    @pl.when(is_diag & (c < n_tiles - 1))
    def _():
        greet(lax.rem(c + 1, n_row), c + 1)

    links = jnp.where(c > 0, 1, 0) + jnp.where(c < n_tiles - 1, 1, 0)
    pl.semaphore_wait(barrier, peers + jnp.where(is_diag, links, 0))

    for load in loads:
        load.wait()
    step = min(64, tile)
    for s in range(2):
        from_narrow = flags[s] == 1

        def choose(n, _, s=s, from_narrow=from_narrow):
            rows = pl.ds(pl.multiple_of(n * step, step), step)
            value = jnp.where(from_narrow, narrow[s, rows, :].astype(F32), wide[s, rows, :])
            wide[s, rows, :] = value
            high, low = halves(value)
            l_high[s, rows, :] = high
            l_low[s, rows, :] = low
            return 0

        lax.fori_loop(0, tile // step, choose, 0)

    holds_below = (r == lax.rem(c + 1, n_row)) & (c < n_tiles - 1)
    below_slot = jnp.minimum(lax.div(c + 1, n_row), 1)
    below_copy = pltpu.make_async_remote_copy(
        src_ref=wide.at[below_slot],
        dst_ref=below,
        send_sem=below_send.at[0],
        recv_sem=below_recv.at[0],
        device_id=(diag_row, c),
        device_id_type=MESH,
    )

    @pl.when(holds_below)
    def _():
        below_copy.start()

    turned_x = jnp.transpose(x_ref[...])
    x_high[...], x_low[...] = halves(turned_x)

    half = tile // 2

    def sends_part(row):
        return (row != diag_row) & (row + n_row >= c + 2)

    @pl.when(is_diag)
    def _():
        turned_g = jnp.transpose(g_ref[...])
        for k in range(chunks):
            g_turned[k] = turned_g[k * width : (k + 1) * width]
        for row in range(n_row):

            @pl.when(jnp.logical_not(sends_part(row)))
            def _(row=row):
                part[row] = jnp.zeros(part.shape[1:], F32)

        rows = lax.broadcasted_iota(jnp.int32, (half, half), 0)
        cols = lax.broadcasted_iota(jnp.int32, (half, half), 1)
        for b in range(2):
            w_full[b * half : (b + 1) * half, b * half : (b + 1) * half] = jnp.zeros((half, half), F32)
        blocks = []
        inverses = []
        for b in range(2):
            at = slice(b * half, (b + 1) * half)
            block = wide[diag_slot, at, at]
            on_diag = jnp.where(rows == cols, block, 0.0)
            down = 1.0 / jnp.sum(on_diag, axis=1, keepdims=True)
            across = 1.0 / jnp.sum(on_diag, axis=0, keepdims=True)
            pairs = (rows == cols + 1) & (lax.rem(rows, 2) == 1)
            inverse = jnp.where(rows == cols, down, 0.0) - jnp.where(pairs, block * down * across, 0.0)
            blocks.append(block)
            inverses.append(inverse)
        size = 2
        while size < half:
            mask = (lax.div(rows, 2 * size) == lax.div(cols, 2 * size)) & (
                lax.rem(lax.div(rows, size), 2) > lax.rem(lax.div(cols, size), 2)
            )
            for b in range(2):
                coupling = jnp.where(mask, blocks[b], 0.0)
                product = dot_full(coupling, inverses[b])
                inverses[b] = inverses[b] - dot_full(inverses[b], product)
            size *= 2
        coupling = wide[diag_slot, half:, :half]
        product = dot_full(coupling, inverses[0])
        corner = -dot_full(inverses[1], product)
        w_full[:half, :half] = inverses[0]
        w_full[:half, half:] = jnp.zeros((half, half), F32)
        w_full[half:, :half] = corner
        w_full[half:, half:] = inverses[1]
        high, low = halves(w_full[...])
        w_high[...] = high
        w_low[...] = low

        @pl.when(c < n_tiles - 1)
        def _():
            below_copy.wait_recv()

            def fold(n, _):
                at = pl.ds(pl.multiple_of(n * (tile // 4), tile // 4), tile // 4)
                high, low = halves(dot3(below[at, :], w_high[...], w_low[...]))
                v_high[at, :] = high
                v_low[at, :] = low
                return 0

            lax.fori_loop(0, 4, fold, 0)

    def chain_copy(k):
        return pltpu.make_async_remote_copy(
            src_ref=y_buf.at[diag_slot, k],
            dst_ref=chain.at[k],
            send_sem=chain_send.at[k],
            recv_sem=chain_recv.at[k],
            device_id=(lax.rem(c + n_row - 1, n_row), jnp.maximum(c - 1, 0)),
            device_id_type=MESH,
        )

    def x_copy(s, k, d):
        return pltpu.make_async_remote_copy(
            src_ref=y_buf.at[s, k],
            dst_ref=y_buf.at[s, k],
            send_sem=x_send.at[d, k],
            recv_sem=row_recv.at[s, k],
            device_id=(r, y * nx + lax.rem(x + d, nx)),
            device_id_type=MESH,
        )

    def y_copy(s, k, d):
        return pltpu.make_async_remote_copy(
            src_ref=y_buf.at[s, k],
            dst_ref=y_buf.at[s, k],
            send_sem=y_send.at[s, d, k],
            recv_sem=row_recv.at[s, k],
            device_id=(r, lax.rem(y + d, ny) * nx + x),
            device_id_type=MESH,
        )

    def part_copy(row, k):
        return pltpu.make_async_remote_copy(
            src_ref=part.at[row, k],
            dst_ref=part.at[row, k],
            send_sem=part_send.at[k],
            recv_sem=part_recv.at[row, k],
            device_id=(diag_row, c),
            device_id_type=MESH,
        )

    for s in (1, 0):
        i = r + n_row * s
        is_source = i == c
        in_source_line = lax.div(i, nx) == y
        takes_part = i >= c + 2
        if s == 1:
            sends_now = takes_part & (r != diag_row) & (r < c + 2)
        else:
            sends_now = takes_part

        @pl.when(is_source)
        def _(s=s):
            def solve(k, _):
                for row in range(n_row):

                    @pl.when(sends_part(row))
                    def _(row=row):
                        part_copy(row, k).wait_recv()

                total = g_turned[k]
                for row in range(n_row):
                    total = total - part[row, k]
                base = dot3(total, w_high[...], w_low[...])
                y_buf[s, k] = base

                @pl.when(c < n_tiles - 1)
                def _():
                    chain_copy(k).wait_recv()
                    y_buf[s, k] = base - dot3(chain[k], v_high[...], v_low[...])

                @pl.when(c > 0)
                def _():
                    chain_copy(k).start()

                for d in range(nx - 1, 0, -1):
                    x_copy(s, k, d).start()
                for d in range(ny - 1, 0, -1):
                    y_copy(s, k, d).start()
                return 0

            lax.fori_loop(0, chunks, solve, 0)

        @pl.when(jnp.logical_not(is_source))
        def _(s=s, in_source_line=in_source_line, takes_part=takes_part, sends_now=sends_now):
            def take(k, _):
                x_copy(s, k, 1).wait_recv()

                @pl.when(in_source_line)
                def _():
                    for d in range(ny - 1, 0, -1):
                        y_copy(s, k, d).start()

                @pl.when(takes_part)
                def _():
                    product = dot3(y_buf[s, k], l_high[s], l_low[s])
                    if s == 0:
                        product = product + part[r, k]
                    part[r, k] = product

                @pl.when(sends_now)
                def _():
                    part_copy(r, k).start()

                return 0

            lax.fori_loop(0, chunks, take, 0)

        block = jnp.concatenate([y_buf[s, k] for k in range(chunks)], axis=0)
        rhs_out[s] = jnp.transpose(block)
        quarter = tile // 4

        def outer(n, _, s=s, i=i):
            at = pl.ds(pl.multiple_of(n * quarter, quarter), quarter)
            value = -dot3(rhs_out[s, at, :], x_high[...], x_low[...])
            rows = lax.broadcasted_iota(jnp.int32, (quarter, tile), 0) + n * quarter
            cols = lax.broadcasted_iota(jnp.int32, (quarter, tile), 1)
            keep = (rows + i * tile) >= (cols + c * tile)
            grad_out[s, at, :] = jnp.where(keep, value, 0.0)
            return 0

        lax.fori_loop(0, 4, outer, 0)
        pltpu.make_async_copy(rhs_out.at[s], rhs_hbm.at[s], store_sem.at[s]).start()
        pltpu.make_async_copy(grad_out.at[s], grad_hbm.at[s], store_sem.at[2 + s]).start()

    @pl.when(holds_below)
    def _():
        below_copy.wait_send()

    for s in (1, 0):
        i = r + n_row * s
        in_source_line = lax.div(i, nx) == y
        takes_part = i >= c + 2
        if s == 1:
            sends_now = takes_part & (r != diag_row) & (r < c + 2)
        else:
            sends_now = takes_part

        @pl.when(i == c)
        def _(s=s):
            def ended(k, _):
                @pl.when(c > 0)
                def _():
                    chain_copy(k).wait_send()

                for d in range(1, nx):
                    x_copy(s, k, d).wait_send()
                return 0

            lax.fori_loop(0, chunks, ended, 0)

        @pl.when(in_source_line)
        def _(s=s):
            def ended(k, _):
                for d in range(1, ny):
                    y_copy(s, k, d).wait_send()
                return 0

            lax.fori_loop(0, chunks, ended, 0)

        @pl.when((i != c) & sends_now)
        def _():
            def ended(k, _):
                part_copy(r, k).wait_send()
                return 0

            lax.fori_loop(0, chunks, ended, 0)

        pltpu.make_async_copy(rhs_out.at[s], rhs_hbm.at[s], store_sem.at[s]).wait()
        pltpu.make_async_copy(grad_out.at[s], grad_hbm.at[s], store_sem.at[2 + s]).wait()


def solution(mesh):
    n_row, n_col = mesh.shape["row"], mesh.shape["col"]
    nx = 4 if n_col == 16 else 2
    ny = n_col // nx

    def body(factor_wide, factor_narrow, flags, forward_solution, solution_grad):
        slots, _, _, _, tile, _ = factor_wide.shape
        rhs = forward_solution.shape[-1]
        chunks = CHUNKS
        width = rhs // chunks
        sizes = (n_row, n_col, nx, ny, tile, rhs, chunks)
        vmem = pltpu.VMEM
        dma = pltpu.SemaphoreType.DMA
        rhs_grad, factor_grad = pl.pallas_call(
            functools.partial(kernel, sizes),
            out_shape=(
                jax.ShapeDtypeStruct((slots, tile, rhs), F32),
                jax.ShapeDtypeStruct((slots, tile, tile), F32),
            ),
            in_specs=[
                pl.BlockSpec(memory_space=pltpu.SMEM),
                pl.BlockSpec(memory_space=pl.ANY),
                pl.BlockSpec(memory_space=pl.ANY),
                pl.BlockSpec(memory_space=pltpu.VMEM),
                pl.BlockSpec(memory_space=pltpu.VMEM),
            ],
            out_specs=(
                pl.BlockSpec(memory_space=pl.ANY),
                pl.BlockSpec(memory_space=pl.ANY),
            ),
            scratch_shapes=[
                vmem((slots, tile, tile), F32),
                vmem((slots, tile, tile), BF16),
                vmem((slots, tile, tile), BF16),
                vmem((slots, tile, tile), BF16),
                vmem((tile, tile), F32),
                vmem((tile, tile), F32),
                vmem((tile, tile), BF16),
                vmem((tile, tile), BF16),
                vmem((tile, tile), BF16),
                vmem((tile, tile), BF16),
                vmem((chunks, width, tile), F32),
                vmem((rhs, tile), BF16),
                vmem((rhs, tile), BF16),
                vmem((slots, chunks, width, tile), F32),
                vmem((chunks, width, tile), F32),
                vmem((n_row, chunks, width, tile), F32),
                vmem((slots, tile, rhs), F32),
                vmem((slots, tile, tile), F32),
                dma((4,)),
                dma((4,)),
                dma((1,)),
                dma((1,)),
                dma((chunks,)),
                dma((chunks,)),
                dma((slots, chunks)),
                dma((nx, chunks)),
                dma((slots, ny, chunks)),
                dma((chunks,)),
                dma((n_row, chunks)),
            ],
            compiler_params=pltpu.CompilerParams(collective_id=0, has_side_effects=True),
        )(
            flags.reshape(slots),
            factor_wide.reshape(slots, tile, tile),
            factor_narrow.reshape(slots, tile, tile),
            forward_solution.reshape(tile, rhs),
            solution_grad.reshape(tile, rhs),
        )
        return (
            rhs_grad[:, None],
            factor_grad.reshape(slots, 1, 1, 1, tile, tile),
        )

    placed = (
        P(None, "row", None, "col", None, None),
        P(None, "row", None, "col", None, None),
        P(None, "row", None, "col"),
        P(None, "col", None, None),
        P(None, "col", None, None),
    )
    return jax.shard_map(
        body,
        mesh=mesh,
        in_specs=placed,
        out_specs=(P(None, "row", None, None), P(None, "row", None, "col", None, None)),
        check_vma=False,
    )
```

time: 1890 us -> 109 us (0.06)
  waiting for transfers between devices: 1580 us -> 0 us
  starting transfers between devices: 163 us -> 0 us
  Pallas kernels: 0 us -> 103 us
  other arithmetic: 56 us -> 0 us
  local copies, waits for them, and re-layouts: 60.9 us -> 4.95 us
    all_gather x16 -> x0, waiting for transfers between devices: 1110 us -> none  [picked(): lax.all_gather(value, axis)]
    all_to_all x15 -> x0, waiting for transfers between devices: 409 us -> none  [sent_to_all(): lax.all_to_all(jnp.broadcast_to(value[None], (size, *value.shape)), axis,...]
    all_to_all x15 -> x0, starting transfers between devices: 129 us -> none  [sent_to_all(): lax.all_to_all(jnp.broadcast_to(value[None], (size, *value.shape)), axis,...]
    pallas_call x0 -> x1, Pallas kernels: none -> 103 us  [body(): pl.pallas_call(functools.partial(kernel, sizes), out_shape=(jax.ShapeDtyp...]
    ppermute x15 -> x0, waiting for transfers between devices: 58.4 us -> none  [from_behind(): lax.ppermute(value, axis, [(i, (i + by) % size) for i in range(size)])]
    reduce_sum x15 -> x0, other arithmetic: 36.3 us -> none  [taken_together(): return sent_to_all(value, axis).sum(axis=0)]
    ppermute x15 -> x0, starting transfers between devices: 33.5 us -> none  [from_behind(): lax.ppermute(value, axis, [(i, (i + by) % size) for i in range(size)])]
    broadcast_in_dim x60 -> x0, local copies, waits for them, and re-layouts: 32.7 us -> none  [the longest x15 21.9 us: sent_to_all(): jnp.broadcast_to(value[None], (size, *value.shape))]
  transfers between devices with their start and end apart: 46 -> 0, of which waited for: 46 -> 0; matrix products, arithmetic and copies ran while one was open for 5% -> 0% of each run, Pallas kernels for 0% -> 0%
where the time goes in v1:
time: 109 us
  Pallas kernels  103 us (94%)
  local copies, waits for them, and re-layouts  4.95 us (5%)
    pallas_call x1, Pallas kernels, body(): pl.pallas_call(functools.partial(kernel, sizes), out_shape=(jax.ShapeDtyp...  103 us
    unnamed x2, local copies, waits for them, and re-layouts  4.95 us

profile of v1, /device:TPU:10, one launch (start us, length us, event | category | flops | bytes accessed | tf_op | source)
XLA Modules:
  0.0 109.0 jit_solution(134176932829426875)
XLA Ops:
  0.6 103.4 %shard_map.68 = (f32[2,512,128]{2,1,0:T(8,128)}, f32[2,512,512]{2,1,0:T(8,128)}) custom-call(s32[2]{0:T(128)} %bitcast.17, f32[2,512,512]{2,1,0:T(8,128)} %bitcast.11, bf16[2,512,512]{2,1,0:T(8,128)(2,1)} %bitcast.13, f32[512,128]{1,0:T(8,128)} %bitcast.15, f32[512,128]{1,0:T(8,128)} %bitcast.16), custom_call_target="tpu_custom_call" | custom-call | tf_op jit(solution)/shard_map/pallas_call | solution.py:405
  104.0 1.9 %copy.11 = f32[2,1,512,128]{3,2,1,0:T(8,128)} copy(f32[2,1,512,128]{3,2,1,0:T(8,128)} %bitcast.14) | data formatting | bytes 1048576
  105.9 3.1 %copy.12 = f32[2,1,1,1,512,512]{5,4,3,2,1,0:T(8,128)} copy(f32[2,1,1,1,512,512]{5,4,3,2,1,0:T(8,128)} %bitcast.12) | data formatting | bytes 4194304

commit v2 on v1

--- a/solution.py
+++ b/solution.py
@@ -49,16 +49,20 @@
     l_high,
     l_low,
     below,
+    below_two,
     w_full,
     w_high,
     w_low,
     v_high,
     v_low,
+    u_high,
+    u_low,
     g_turned,
     x_high,
     x_low,
     y_buf,
     chain,
+    chain_two,
     part,
     rhs_out,
     grad_out,
@@ -68,6 +72,8 @@
     below_recv,
     chain_send,
     chain_recv,
+    two_send,
+    two_recv,
     row_recv,
     x_send,
     y_send,
@@ -84,6 +90,9 @@
     diag_row = lax.rem(c, n_row)
     diag_slot = lax.div(c, n_row)
     is_diag = r == diag_row
+    last_two = n_tiles * 5 // 8
+    with_two = c <= last_two
+    first = c + jnp.where(with_two, 3, 2)
 
     loads = [
         pltpu.make_async_copy(wide_hbm.at[s], wide.at[s], load_sem.at[s]) for s in range(2)
@@ -106,6 +115,9 @@
         greet(lax.rem(r + d, n_row), c)
     peers = nx + ny + n_row - 3
 
+    gives_two = is_diag & (c >= 2) & (c <= last_two + 2)
+    takes_two = is_diag & with_two
+
     @pl.when(is_diag & (c > 0))
     def _():
         greet(lax.rem(c + n_row - 1, n_row), c - 1)
@@ -114,8 +126,17 @@
     def _():
         greet(lax.rem(c + 1, n_row), c + 1)
 
+    @pl.when(gives_two)
+    def _():
+        greet(lax.rem(c + n_row - 2, n_row), c - 2)
+
+    @pl.when(takes_two)
+    def _():
+        greet(lax.rem(c + 2, n_row), c + 2)
+
     links = jnp.where(c > 0, 1, 0) + jnp.where(c < n_tiles - 1, 1, 0)
-    pl.semaphore_wait(barrier, peers + jnp.where(is_diag, links, 0))
+    links = jnp.where(is_diag, links, 0) + jnp.where(gives_two, 1, 0) + jnp.where(takes_two, 1, 0)
+    pl.semaphore_wait(barrier, peers + links)
 
     for load in loads:
         load.wait()
@@ -145,9 +166,24 @@
         device_id_type=MESH,
     )
 
+    holds_two = (r == lax.rem(c + 2, n_row)) & with_two
+    two_slot = jnp.minimum(lax.div(c + 2, n_row), 1)
+    below_two_copy = pltpu.make_async_remote_copy(
+        src_ref=wide.at[two_slot],
+        dst_ref=below_two,
+        send_sem=below_send.at[1],
+        recv_sem=below_recv.at[1],
+        device_id=(diag_row, c),
+        device_id_type=MESH,
+    )
+
     @pl.when(holds_below)
     def _():
         below_copy.start()
+
+    @pl.when(holds_two)
+    def _():
+        below_two_copy.start()
 
     turned_x = jnp.transpose(x_ref[...])
     x_high[...], x_low[...] = halves(turned_x)
@@ -155,7 +191,7 @@
     half = tile // 2
 
     def sends_part(row):
-        return (row != diag_row) & (row + n_row >= c + 2)
+        return (row != diag_row) & (row + n_row >= first)
 
     @pl.when(is_diag)
     def _():
@@ -205,18 +241,15 @@
         w_high[...] = high
         w_low[...] = low
 
-        @pl.when(c < n_tiles - 1)
-        def _():
-            below_copy.wait_recv()
-
-            def fold(n, _):
-                at = pl.ds(pl.multiple_of(n * (tile // 4), tile // 4), tile // 4)
-                high, low = halves(dot3(below[at, :], w_high[...], w_low[...]))
-                v_high[at, :] = high
-                v_low[at, :] = low
-                return 0
-
-            lax.fori_loop(0, 4, fold, 0)
+    def fold(source, high_ref, low_ref):
+        def some(n, _):
+            at = pl.ds(pl.multiple_of(n * (tile // 4), tile // 4), tile // 4)
+            high, low = halves(dot3(source[at, :], w_high[...], w_low[...]))
+            high_ref[at, :] = high
+            low_ref[at, :] = low
+            return 0
+
+        lax.fori_loop(0, 4, some, 0)
 
     def chain_copy(k):
         return pltpu.make_async_remote_copy(
@@ -228,13 +261,23 @@
             device_id_type=MESH,
         )
 
-    def x_copy(s, k, d):
+    def two_copy(k):
+        return pltpu.make_async_remote_copy(
+            src_ref=y_buf.at[diag_slot, k],
+            dst_ref=chain_two.at[k],
+            send_sem=two_send.at[k],
+            recv_sem=two_recv.at[k],
+            device_id=(lax.rem(c + n_row - 2, n_row), jnp.maximum(c - 2, 0)),
+            device_id_type=MESH,
+        )
+
+    def x_copy(s, k):
         return pltpu.make_async_remote_copy(
             src_ref=y_buf.at[s, k],
             dst_ref=y_buf.at[s, k],
-            send_sem=x_send.at[d, k],
+            send_sem=x_send.at[s, k],
             recv_sem=row_recv.at[s, k],
-            device_id=(r, y * nx + lax.rem(x + d, nx)),
+            device_id=(r, y * nx + lax.rem(x + 1, nx)),
             device_id_type=MESH,
         )
 
@@ -242,7 +285,7 @@
         return pltpu.make_async_remote_copy(
             src_ref=y_buf.at[s, k],
             dst_ref=y_buf.at[s, k],
-            send_sem=y_send.at[s, d, k],
+            send_sem=y_send.at[d, k],
             recv_sem=row_recv.at[s, k],
             device_id=(r, lax.rem(y + d, ny) * nx + x),
             device_id_type=MESH,
@@ -258,18 +301,32 @@
             device_id_type=MESH,
         )
 
-    for s in (1, 0):
+    def roles(s):
         i = r + n_row * s
-        is_source = i == c
-        in_source_line = lax.div(i, nx) == y
-        takes_part = i >= c + 2
+        takes_part = i >= first
         if s == 1:
-            sends_now = takes_part & (r != diag_row) & (r < c + 2)
+            sends_now = takes_part & (r != diag_row) & (r < first)
         else:
             sends_now = takes_part
+        passes_on = lax.rem(x + 1, nx) != lax.rem(i, nx)
+        return i, takes_part, sends_now, passes_on
+
+    for s in (1, 0):
+        i, takes_part, sends_now, passes_on = roles(s)
+        is_source = i == c
 
         @pl.when(is_source)
         def _(s=s):
+            @pl.when(c < n_tiles - 1)
+            def _():
+                below_copy.wait_recv()
+                fold(below, v_high, v_low)
+
+            @pl.when(with_two)
+            def _():
+                below_two_copy.wait_recv()
+                fold(below_two, u_high, u_low)
+
             def solve(k, _):
                 for row in range(n_row):
 
@@ -280,35 +337,42 @@
                 total = g_turned[k]
                 for row in range(n_row):
                     total = total - part[row, k]
-                base = dot3(total, w_high[...], w_low[...])
-                y_buf[s, k] = base
+                y_buf[s, k] = dot3(total, w_high[...], w_low[...])
+
+                @pl.when(with_two)
+                def _():
+                    two_copy(k).wait_recv()
+                    y_buf[s, k] = y_buf[s, k] - dot3(chain_two[k], u_high[...], u_low[...])
 
                 @pl.when(c < n_tiles - 1)
                 def _():
                     chain_copy(k).wait_recv()
-                    y_buf[s, k] = base - dot3(chain[k], v_high[...], v_low[...])
+                    y_buf[s, k] = y_buf[s, k] - dot3(chain[k], v_high[...], v_low[...])
 
                 @pl.when(c > 0)
                 def _():
                     chain_copy(k).start()
 
-                for d in range(nx - 1, 0, -1):
-                    x_copy(s, k, d).start()
                 for d in range(ny - 1, 0, -1):
                     y_copy(s, k, d).start()
+
+                @pl.when(gives_two)
+                def _():
+                    two_copy(k).start()
+
+                x_copy(s, k).start()
                 return 0
 
             lax.fori_loop(0, chunks, solve, 0)
 
         @pl.when(jnp.logical_not(is_source))
-        def _(s=s, in_source_line=in_source_line, takes_part=takes_part, sends_now=sends_now):
+        def _(s=s, takes_part=takes_part, sends_now=sends_now, passes_on=passes_on):
             def take(k, _):
-                x_copy(s, k, 1).wait_recv()
-
-                @pl.when(in_source_line)
-                def _():
-                    for d in range(ny - 1, 0, -1):
-                        y_copy(s, k, d).start()
+                x_copy(s, k).wait_recv()
+
+                @pl.when(passes_on)
+                def _():
+                    x_copy(s, k).start()
 
                 @pl.when(takes_part)
                 def _():
@@ -346,14 +410,12 @@
     def _():
         below_copy.wait_send()
 
+    @pl.when(holds_two)
+    def _():
+        below_two_copy.wait_send()
+
     for s in (1, 0):
-        i = r + n_row * s
-        in_source_line = lax.div(i, nx) == y
-        takes_part = i >= c + 2
-        if s == 1:
-            sends_now = takes_part & (r != diag_row) & (r < c + 2)
-        else:
-            sends_now = takes_part
+        i, takes_part, sends_now, passes_on = roles(s)
 
         @pl.when(i == c)
         def _(s=s):
@@ -362,17 +424,20 @@
                 def _():
                     chain_copy(k).wait_send()
 
-                for d in range(1, nx):
-                    x_copy(s, k, d).wait_send()
+                @pl.when(gives_two)
+                def _():
+                    two_copy(k).wait_send()
+
+                for d in range(1, ny):
+                    y_copy(s, k, d).wait_send()
                 return 0
 
             lax.fori_loop(0, chunks, ended, 0)
 
-        @pl.when(in_source_line)
+        @pl.when(passes_on)
         def _(s=s):
             def ended(k, _):
-                for d in range(1, ny):
-                    y_copy(s, k, d).wait_send()
+                x_copy(s, k).wait_send()
                 return 0
 
             lax.fori_loop(0, chunks, ended, 0)
@@ -391,7 +456,7 @@
 
 def solution(mesh):
     n_row, n_col = mesh.shape["row"], mesh.shape["col"]
-    nx = 4 if n_col == 16 else 2
+    nx = 4 if n_col > 4 else 2
     ny = n_col // nx
 
     def body(factor_wide, factor_narrow, flags, forward_solution, solution_grad):
@@ -426,6 +491,9 @@
                 vmem((slots, tile, tile), BF16),
                 vmem((tile, tile), F32),
                 vmem((tile, tile), F32),
+                vmem((tile, tile), F32),
+                vmem((tile, tile), BF16),
+                vmem((tile, tile), BF16),
                 vmem((tile, tile), BF16),
                 vmem((tile, tile), BF16),
                 vmem((tile, tile), BF16),
@@ -435,18 +503,21 @@
                 vmem((rhs, tile), BF16),
                 vmem((slots, chunks, width, tile), F32),
                 vmem((chunks, width, tile), F32),
+                vmem((chunks, width, tile), F32),
                 vmem((n_row, chunks, width, tile), F32),
                 vmem((slots, tile, rhs), F32),
                 vmem((slots, tile, tile), F32),
                 dma((4,)),
                 dma((4,)),
-                dma((1,)),
-                dma((1,)),
+                dma((2,)),
+                dma((2,)),
+                dma((chunks,)),
+                dma((chunks,)),
                 dma((chunks,)),
                 dma((chunks,)),
                 dma((slots, chunks)),
-                dma((nx, chunks)),
-                dma((slots, ny, chunks)),
+                dma((slots, chunks)),
+                dma((ny, chunks)),
                 dma((chunks,)),
                 dma((n_row, chunks)),
             ],

time: 109 us -> 106 us (0.972)
  the two profiles are of different devices: /device:TPU:10 before, /device:TPU:14 now
where the time goes in v2:
time: 106 us; the launch traced here: 105 us
  Pallas kernels  99.7 us (94%)
  local copies, waits for them, and re-layouts  4.95 us (5%)
    pallas_call x1, Pallas kernels, body(): pl.pallas_call(functools.partial(kernel, sizes), out_shape=(jax.ShapeDtyp...  99.7 us
    unnamed x2, local copies, waits for them, and re-layouts  4.95 us

profile of v2, /device:TPU:14, one launch (start us, length us, event | category | flops | bytes accessed | tf_op | source)
XLA Modules:
  0.0 105.3 jit_solution(3225775674761361362)
XLA Ops:
  0.6 99.7 %shard_map.68 = (f32[2,512,128]{2,1,0:T(8,128)}, f32[2,512,512]{2,1,0:T(8,128)}) custom-call(s32[2]{0:T(128)} %bitcast.17, f32[2,512,512]{2,1,0:T(8,128)} %bitcast.11, bf16[2,512,512]{2,1,0:T(8,128)(2,1)} %bitcast.13, f32[512,128]{1,0:T(8,128)} %bitcast.15, f32[512,128]{1,0:T(8,128)} %bitcast.16), custom_call_target="tpu_custom_call" | custom-call | tf_op jit(solution)/shard_map/pallas_call | solution.py:470
  100.4 1.9 %copy.11 = f32[2,1,512,128]{3,2,1,0:T(8,128)} copy(f32[2,1,512,128]{3,2,1,0:T(8,128)} %bitcast.14) | data formatting | bytes 1048576
  102.3 3.1 %copy.12 = f32[2,1,1,1,512,512]{5,4,3,2,1,0:T(8,128)} copy(f32[2,1,1,1,512,512]{5,4,3,2,1,0:T(8,128)} %bitcast.12) | data formatting | bytes 4194304

commit v3 on v2

--- a/solution.py
+++ b/solution.py
@@ -42,8 +42,8 @@
     narrow_hbm,
     x_ref,
     g_ref,
-    rhs_hbm,
-    grad_hbm,
+    rhs_out,
+    grad_out,
     wide,
     narrow,
     l_high,
@@ -64,10 +64,9 @@
     chain,
     chain_two,
     part,
-    rhs_out,
-    grad_out,
+    sums,
+    totals,
     load_sem,
-    store_sem,
     below_send,
     below_recv,
     chain_send,
@@ -78,7 +77,8 @@
     x_send,
     y_send,
     part_send,
-    part_recv,
+    sums_recv,
+    totals_recv,
 ):
     n_row, n_col, nx, ny, tile, rhs, chunks = sizes
     n_tiles = 2 * n_row
@@ -190,20 +190,11 @@
 
     half = tile // 2
 
-    def sends_part(row):
-        return (row != diag_row) & (row + n_row >= first)
-
     @pl.when(is_diag)
     def _():
         turned_g = jnp.transpose(g_ref[...])
         for k in range(chunks):
             g_turned[k] = turned_g[k * width : (k + 1) * width]
-        for row in range(n_row):
-
-            @pl.when(jnp.logical_not(sends_part(row)))
-            def _(row=row):
-                part[row] = jnp.zeros(part.shape[1:], F32)
-
         rows = lax.broadcasted_iota(jnp.int32, (half, half), 0)
         cols = lax.broadcasted_iota(jnp.int32, (half, half), 1)
         for b in range(2):
@@ -271,13 +262,13 @@
             device_id_type=MESH,
         )
 
-    def x_copy(s, k):
+    def x_copy(s, k, d):
         return pltpu.make_async_remote_copy(
             src_ref=y_buf.at[s, k],
             dst_ref=y_buf.at[s, k],
-            send_sem=x_send.at[s, k],
+            send_sem=x_send.at[s, d, k],
             recv_sem=row_recv.at[s, k],
-            device_id=(r, y * nx + lax.rem(x + 1, nx)),
+            device_id=(r, y * nx + lax.rem(x + d, nx)),
             device_id_type=MESH,
         )
 
@@ -291,32 +282,60 @@
             device_id_type=MESH,
         )
 
-    def part_copy(row, k):
+    def part_copy(s, k, ends):
+        if ends:
+            dst, sem, row = totals.at[k], totals_recv.at[k], diag_row
+        else:
+            slot = jnp.where(r > 0, s, max(s - 1, 0))
+            dst, sem, row = sums.at[slot, k], sums_recv.at[slot, k], lax.rem(r + n_row - 1, n_row)
         return pltpu.make_async_remote_copy(
-            src_ref=part.at[row, k],
-            dst_ref=part.at[row, k],
-            send_sem=part_send.at[k],
-            recv_sem=part_recv.at[row, k],
-            device_id=(diag_row, c),
+            src_ref=part.at[s, k],
+            dst_ref=dst,
+            send_sem=part_send.at[s, k],
+            recv_sem=sem,
+            device_id=(row, c),
             device_id_type=MESH,
         )
 
-    def roles(s):
+    def sums_copy(s, k):
+        return pltpu.make_async_remote_copy(
+            src_ref=part.at[s, k],
+            dst_ref=sums.at[s, k],
+            send_sem=part_send.at[s, k],
+            recv_sem=sums_recv.at[s, k],
+            device_id=(lax.rem(r + n_row - 1, n_row), c),
+            device_id_type=MESH,
+        )
+
+    def place(s):
         i = r + n_row * s
-        takes_part = i >= first
-        if s == 1:
-            sends_now = takes_part & (r != diag_row) & (r < first)
-        else:
-            sends_now = takes_part
-        passes_on = lax.rem(x + 1, nx) != lax.rem(i, nx)
-        return i, takes_part, sends_now, passes_on
+        from_x, from_y = lax.rem(i, nx), lax.div(i, nx)
+        serves_line = (x == from_x) & ((y != from_y) | (i == 0))
+        passes_on = (y == from_y) & (i > 0) & (lax.rem(x + 1, nx) != from_x)
+        return i, i >= first, serves_line, passes_on
+
+    def send_x(s, k, serves_line, passes_on, act):
+        @pl.when(serves_line)
+        def _():
+            for d in range(1, nx):
+                act(x_copy(s, k, d))
+
+        @pl.when(passes_on)
+        def _():
+            act(x_copy(s, k, 1))
+
+    def start(copy):
+        copy.start()
+
+    def wait_sent(copy):
+        copy.wait_send()
 
     for s in (1, 0):
-        i, takes_part, sends_now, passes_on = roles(s)
+        i, takes_part, serves_line, passes_on = place(s)
         is_source = i == c
 
         @pl.when(is_source)
-        def _(s=s):
+        def _(s=s, serves_line=serves_line, passes_on=passes_on):
             @pl.when(c < n_tiles - 1)
             def _():
                 below_copy.wait_recv()
@@ -328,16 +347,12 @@
                 fold(below_two, u_high, u_low)
 
             def solve(k, _):
-                for row in range(n_row):
-
-                    @pl.when(sends_part(row))
-                    def _(row=row):
-                        part_copy(row, k).wait_recv()
-
-                total = g_turned[k]
-                for row in range(n_row):
-                    total = total - part[row, k]
-                y_buf[s, k] = dot3(total, w_high[...], w_low[...])
+                @pl.when(first < n_tiles)
+                def _():
+                    part_copy(0, k, True).wait_recv()
+                    g_turned[k] = g_turned[k] - totals[k]
+
+                y_buf[s, k] = dot3(g_turned[k], w_high[...], w_low[...])
 
                 @pl.when(with_two)
                 def _():
@@ -360,30 +375,33 @@
                 def _():
                     two_copy(k).start()
 
-                x_copy(s, k).start()
+                send_x(s, k, serves_line, passes_on, start)
                 return 0
 
             lax.fori_loop(0, chunks, solve, 0)
 
         @pl.when(jnp.logical_not(is_source))
-        def _(s=s, takes_part=takes_part, sends_now=sends_now, passes_on=passes_on):
+        def _(s=s, i=i, takes_part=takes_part, serves_line=serves_line, passes_on=passes_on):
             def take(k, _):
-                x_copy(s, k).wait_recv()
-
-                @pl.when(passes_on)
-                def _():
-                    x_copy(s, k).start()
+                x_copy(s, k, 1).wait_recv()
+                send_x(s, k, serves_line, passes_on, start)
 
                 @pl.when(takes_part)
                 def _():
-                    product = dot3(y_buf[s, k], l_high[s], l_low[s])
-                    if s == 0:
-                        product = product + part[r, k]
-                    part[r, k] = product
-
-                @pl.when(sends_now)
-                def _():
-                    part_copy(r, k).start()
+                    part[s, k] = dot3(y_buf[s, k], l_high[s], l_low[s])
+
+                    @pl.when(i < n_tiles - 1)
+                    def _():
+                        sums_copy(s, k).wait_recv()
+                        part[s, k] = part[s, k] + sums[s, k]
+
+                    @pl.when(i > first)
+                    def _():
+                        part_copy(s, k, False).start()
+
+                    @pl.when(i == first)
+                    def _():
+                        part_copy(s, k, True).start()
 
                 return 0
 
@@ -393,18 +411,22 @@
         rhs_out[s] = jnp.transpose(block)
         quarter = tile // 4
 
-        def outer(n, _, s=s, i=i):
-            at = pl.ds(pl.multiple_of(n * quarter, quarter), quarter)
-            value = -dot3(rhs_out[s, at, :], x_high[...], x_low[...])
-            rows = lax.broadcasted_iota(jnp.int32, (quarter, tile), 0) + n * quarter
-            cols = lax.broadcasted_iota(jnp.int32, (quarter, tile), 1)
-            keep = (rows + i * tile) >= (cols + c * tile)
-            grad_out[s, at, :] = jnp.where(keep, value, 0.0)
-            return 0
-
-        lax.fori_loop(0, 4, outer, 0)
-        pltpu.make_async_copy(rhs_out.at[s], rhs_hbm.at[s], store_sem.at[s]).start()
-        pltpu.make_async_copy(grad_out.at[s], grad_hbm.at[s], store_sem.at[2 + s]).start()
+        @pl.when(i < c)
+        def _(s=s):
+            grad_out[s] = jnp.zeros((tile, tile), F32)
+
+        @pl.when(i >= c)
+        def _(s=s, i=i):
+            def outer(n, _):
+                at = pl.ds(pl.multiple_of(n * quarter, quarter), quarter)
+                value = -dot3(rhs_out[s, at, :], x_high[...], x_low[...])
+                rows = lax.broadcasted_iota(jnp.int32, (quarter, tile), 0) + n * quarter
+                cols = lax.broadcasted_iota(jnp.int32, (quarter, tile), 1)
+                keep = (rows + i * tile) >= (cols + c * tile)
+                grad_out[s, at, :] = jnp.where(keep, value, 0.0)
+                return 0
+
+            lax.fori_loop(0, 4, outer, 0)
 
     @pl.when(holds_below)
     def _():
@@ -415,7 +437,7 @@
         below_two_copy.wait_send()
 
     for s in (1, 0):
-        i, takes_part, sends_now, passes_on = roles(s)
+        i, takes_part, serves_line, passes_on = place(s)
 
         @pl.when(i == c)
         def _(s=s):
@@ -434,24 +456,19 @@
 
             lax.fori_loop(0, chunks, ended, 0)
 
-        @pl.when(passes_on)
+        def ended_line(k, _, s=s, serves_line=serves_line, passes_on=passes_on):
+            send_x(s, k, serves_line, passes_on, wait_sent)
+            return 0
+
+        lax.fori_loop(0, chunks, ended_line, 0)
+
+        @pl.when((i != c) & takes_part)
         def _(s=s):
             def ended(k, _):
-                x_copy(s, k).wait_send()
+                sums_copy(s, k).wait_send()
                 return 0
 
             lax.fori_loop(0, chunks, ended, 0)
-
-        @pl.when((i != c) & sends_now)
-        def _():
-            def ended(k, _):
-                part_copy(r, k).wait_send()
-                return 0
-
-            lax.fori_loop(0, chunks, ended, 0)
-
-        pltpu.make_async_copy(rhs_out.at[s], rhs_hbm.at[s], store_sem.at[s]).wait()
-        pltpu.make_async_copy(grad_out.at[s], grad_hbm.at[s], store_sem.at[2 + s]).wait()
 
 
 def solution(mesh):
@@ -470,8 +487,8 @@
         rhs_grad, factor_grad = pl.pallas_call(
             functools.partial(kernel, sizes),
             out_shape=(
-                jax.ShapeDtypeStruct((slots, tile, rhs), F32),
-                jax.ShapeDtypeStruct((slots, tile, tile), F32),
+                pltpu.VMEM((slots, tile, rhs), F32),
+                pltpu.VMEM((slots, tile, tile), F32),
             ),
             in_specs=[
                 pl.BlockSpec(memory_space=pltpu.SMEM),
@@ -481,8 +498,8 @@
                 pl.BlockSpec(memory_space=pltpu.VMEM),
             ],
             out_specs=(
-                pl.BlockSpec(memory_space=pl.ANY),
-                pl.BlockSpec(memory_space=pl.ANY),
+                pl.BlockSpec(memory_space=pltpu.VMEM),
+                pl.BlockSpec(memory_space=pltpu.VMEM),
             ),
             scratch_shapes=[
                 vmem((slots, tile, tile), F32),
@@ -504,10 +521,9 @@
                 vmem((slots, chunks, width, tile), F32),
                 vmem((chunks, width, tile), F32),
                 vmem((chunks, width, tile), F32),
-                vmem((n_row, chunks, width, tile), F32),
-                vmem((slots, tile, rhs), F32),
-                vmem((slots, tile, tile), F32),
-                dma((4,)),
+                vmem((slots, chunks, width, tile), F32),
+                vmem((slots, chunks, width, tile), F32),
+                vmem((chunks, width, tile), F32),
                 dma((4,)),
                 dma((2,)),
                 dma((2,)),
@@ -516,10 +532,11 @@
                 dma((chunks,)),
                 dma((chunks,)),
                 dma((slots, chunks)),
+                dma((slots, nx, chunks)),
+                dma((ny, chunks)),
                 dma((slots, chunks)),
-                dma((ny, chunks)),
+                dma((slots, chunks)),
                 dma((chunks,)),
-                dma((n_row, chunks)),
             ],
             compiler_params=pltpu.CompilerParams(collective_id=0, has_side_effects=True),
         )(

time: 106 us -> 96.8 us (0.913)
  the two profiles are of different devices: /device:TPU:14 before, /device:TPU:10 now
where the time goes in v3:
time: 96.8 us; the launch traced here: 95 us
  Pallas kernels  92.2 us (95%)
  local copies, waits for them, and re-layouts  2.11 us (2%)
    pallas_call x1, Pallas kernels, body(): pl.pallas_call(functools.partial(kernel, sizes), out_shape=(pltpu.VMEM((s...  92.2 us
    unnamed x2, local copies, waits for them, and re-layouts  2.11 us

profile of v3, /device:TPU:10, one launch (start us, length us, event | category | flops | bytes accessed | tf_op | source)
XLA Modules:
  0.0 95.0 jit_solution(9242392206827151026)
XLA Ops:
  0.6 92.2 %shard_map.68 = (f32[2,512,128]{2,1,0:T(8,128)S(1)}, f32[2,512,512]{2,1,0:T(8,128)S(1)}) custom-call(s32[2]{0:T(128)} %bitcast.17, f32[2,512,512]{2,1,0:T(8,128)} %bitcast.13, bf16[2,512,512]{2,1,0:T(8,128)(2,1)} %bitcast.14, f32[512,128]{1,0:T(8,128)} %bitcast.15, f32[512,128]{1,0:T(8,128)} %bitcast.16), custom_call_target="tpu_custom_call" | custom-call | tf_op jit(solution)/shard_map/pallas_call | solution.py:487
  92.9 0.8 copy.11
  93.7 1.3 %copy.12 = f32[2,1,1,1,512,512]{5,4,3,2,1,0:T(8,128)} copy(f32[2,1,1,1,512,512]{5,4,3,2,1,0:T(8,128)S(1)} %bitcast.11) | data formatting | bytes 4194304
